TPU v7x, 128 devices: a whole 4x4x4 slice. The times are simulated.
128 devices in a mesh: dp: 8 (over x, y_lo), vocab: 16 (over z, y_hi, core).
Axes of the slice: x: 4, y: 4 (y_hi: 2, y_lo: 2; y = y_hi * 2 + y_lo), z: 4, core: 2. Of those that a mesh axis runs over, the one named last changes fastest.
Arguments:
- hidden: bfloat16 [8192, 5120], P(('dp', 'vocab')), may hold values from -100 to 100
- tokens: int32 [8192], P('dp'), may hold values from 0 to 18431
- old_weight: bfloat16 [18432, 5120], P('vocab'), may hold values from -1 to 1
- new_weight: bfloat16 [18432, 5120], P('dp', 'vocab'), may hold values from -6 to 6
Outputs:
- logprob: float32 [8192], P(('dp', 'vocab'))
- engine_weight: bfloat16 [18432, 5120], P('vocab')
All inputs are finite; a program needn't handle non-finite values.
Results may differ from a plain program's by a relative error of at most 0.001.
Values may be sent and summed in bfloat16 or wider, within the bound.
A program may use at most 128 MiB of HBM per device.

v0:
```python
import jax
import jax.numpy as jnp
from jax import lax
from jax.sharding import Mesh
from jax.sharding import PartitionSpec as P

DP = ("dp_0", "dp_1")
DP_VOCAB = ("dp_0", "dp_1", "vocab")


def sent_together(arrays, axis, split_dim, concat_dim, along):
    ends, at = ([], 0)
    for a in arrays[:-1]:
        at += a.shape[along]
        ends.append(at)
    both = jnp.concatenate(arrays, axis=along)
    return tuple(
        jnp.split(
            lax.all_to_all(both, axis, split_axis=split_dim, concat_axis=concat_dim, tiled=True),
            ends,
            axis=along,
        )
    )


def whole_of(shard, axes, dim):
    if not axes:
        return shard
    nearer = lax.all_gather(shard, axes[-1], axis=dim, tiled=True)
    return whole_of(nearer, axes[:-1], dim)


def on_device(hidden, tokens, old_weight, new_weight):
    ranks = lax.axis_size("vocab")
    rank = lax.axis_index("vocab")
    vocab_rows = old_weight.shape[0]
    first_id = rank * vocab_rows
    own_rows = hidden.shape[0]
    logits = lax.dot_general(
        lax.all_gather(hidden, "vocab", axis=0, tiled=True),
        old_weight,
        (((1,), (1,)), ((), ())),
        preferred_element_type=jnp.float32,
    )
    highest = jnp.max(logits, axis=1)
    summed = jnp.sum(jnp.exp(logits - highest[:, None]), axis=1)
    wanted = tokens - first_id
    columns = lax.broadcasted_iota(jnp.int32, logits.shape, 1)
    target = jnp.sum(jnp.where(columns == wanted[:, None], logits, 0.0), axis=1)
    stats = jnp.stack([highest, summed, target], axis=0)
    highest, summed, target = (stats[0], stats[1], stats[2])
    shaped = (
        highest.reshape(ranks, own_rows),
        summed.reshape(ranks, own_rows),
        target.reshape(ranks, own_rows),
    )
    got_high, got_sum, got_target = sent_together(
        (shaped[0], shaped[1], shaped[2]), "vocab", 0, 0, 1
    )
    highest = jnp.max(got_high, axis=0)
    summed = jnp.sum(got_sum * jnp.exp(got_high - highest[None, :]), axis=0)
    target = jnp.sum(got_target, axis=0)
    logprob = target - highest - jnp.log(summed)
    replicas = lax.axis_size(DP)
    trainer_cols = new_weight.shape[1]
    owned = lax.all_to_all(
        lax.all_to_all(new_weight, DP, split_axis=1, concat_axis=0, tiled=True),
        "vocab",
        split_axis=0,
        concat_axis=1,
        tiled=True,
    )
    owner_count = owned.shape[0]
    shaped_pieces = owned.reshape(owner_count, ranks, 1, trainer_cols // replicas)
    complete = whole_of(shaped_pieces, DP, 2)
    engine_weight = complete.reshape(owner_count, ranks * trainer_cols)
    return (logprob, engine_weight)


def solution(mesh):
    finer = Mesh(mesh.devices.reshape(4, 2, mesh.shape["vocab"]), ("dp_0", "dp_1", "vocab"))
    return jax.shard_map(
        on_device,
        mesh=finer,
        in_specs=(P(DP_VOCAB, None), P(DP), P("vocab", None), P(DP, "vocab")),
        out_specs=(P(DP_VOCAB), P("vocab", None)),
        check_vma=False,
    )
```

profile of v0, /device:TPU:1, one launch (start us, length us, event | category | flops | bytes accessed | tf_op | source)
XLA Modules:
  0.0 325.5 jit_solution(2934551947676968886)
XLA Ops:
  7.2 0.0 all-gather.9.cloned.1.call-start
  7.2 24.7 %all_to_all.44 = bf16[2304,8,40]{0,2,1:T(8,128)(2,1)S(1)} all-to-all(bf16[2304,8,40]{0,2,1:T(8,128)(2,1)} %bitcast.16), channel_id=1, replica_groups=mesh['dp_0'=4,'dp_1'=2,'vocab'=16] {'dp_0','dp_1'}, dimensions={1} | all-to-all | bytes 2949120 | tf_op jit(solution)/shard_map/all_to_all | solution.py:67
  31.9 0.2 copy.9
  32.2 0.5 all_to_all.38
  32.7 0.3 copy.10
  33.0 31.0 %all_to_all.45 = bf16[16,1152,40]{1,2,0:T(8,128)(2,1)S(1)} all-to-all(bf16[16,1152,40]{1,2,0:T(8,128)(2,1)S(1)} %copy.10), channel_id=1, replica_groups=mesh['dp_0'=4,'dp_1'=2,'vocab'=16] {'vocab'}, dimensions={0} | all-to-all | bytes 2949120 | tf_op jit(solution)/shard_map/all_to_all | solution.py:66
  64.0 1.3 copy.11
  65.2 0.0 all-gather.9.cloned.1.call-update
  65.2 0.0 copy-start
  65.3 0.0 all-gather.5.cloned.1.call-start
  65.3 0.7 all-gather.5.cloned.1.call-update
  66.0 0.0 all-gather.7.cloned.1.call-start
  66.1 40.3 %all-gather.9.cloned.1.call-done = bf16[1152,16,80]{0,1,2:T(8,128)(2,1)} async-done(((bf16[1152,16,40]{0,1,2:T(8,128)(2,1)}), bf16[1152,16,80]{0,1,2:T(8,128)(2,1)}) %all-gather.9.cloned.1.call-update) | async-done | bytes 2949136 | tf_op jit(solution)/shard_map/all_gather | solution.py:29
  106.3 4.0 %copy.12 = bf16[1152,16,80]{0,2,1:T(8,128)(2,1)} copy(bf16[1152,16,80]{0,1,2:T(8,128)(2,1)} %all-gather.9.cloned.1.call-done) | data formatting | bytes 5898240 | tf_op jit(solution)/shard_map/all_gather | solution.py:29
  110.3 0.0 all-gather.7.cloned.1.call-update
  110.3 0.0 copy-done
  110.4 81.7 %all-gather.5.cloned.1.call-done = bf16[1024,5120]{1,0:T(8,128)(2,1)} async-done(((bf16[64,5120]{1,0:T(8,128)(2,1)}), bf16[1024,5120]{1,0:T(8,128)(2,1)}) %all-gather.5.cloned.1.call-update) | async-done | bytes 10485776 | tf_op jit(solution)/shard_map/all_gather | solution.py:40
  192.1 19.5 %fusion.1 = (f32[1024]{0:T(1024)S(1)}, f32[1024,1152]{1,0:T(8,128)}) fusion(bf16[1024,5120]{1,0:T(8,128)(2,1)} %all-gather.5.cloned.1.call-done, bf16[1152,5120]{1,0:T(8,128)(2,1)} %param.6), kind=kOutput, calls=%fused_computation.11 | convolution fusion | flops 12080774144 | bytes 27004928 | tf_op jit(solution)/shard_map/dot_general | solution.py:39
  211.5 0.1 reshape_squeeze_stack.9
  211.6 3.1 exponential_reduce_fusion
  214.8 0.1 reshape_squeeze_stack.10
  214.8 0.1 reshape_squeeze_stack.11
  214.9 0.1 pad_maximum_fusion
  215.0 10.4 %all_to_all.46 = f32[16,1,192]{2,1,0:T(1,128)S(1)} all-to-all(f32[16,1,192]{2,1,0:T(1,128)S(1)} %all_to_all.32), channel_id=1, replica_groups=mesh['dp_0'=4,'dp_1'=2,'vocab'=16] {'vocab'}, dimensions={0} | all-to-all | bytes 24576 | tf_op jit(solution)/shard_map/all_to_all | solution.py:19
  225.4 0.1 slice_reduce_fusion
  225.5 0.5 log_subtract_fusion
  226.0 76.7 %all-gather.7.cloned.1.call-done = bf16[1152,16,8,40]{0,3,2,1:T(8,128)(2,1)} async-done(((bf16[1152,16,2,40]{0,3,2,1:T(8,128)(2,1)}), bf16[1152,16,8,40]{0,3,2,1:T(8,128)(2,1)}) %all-gather.7.cloned.1.call-update) | async-done | bytes 11796496 | tf_op jit(solution)/shard_map/all_gather | solution.py:29
  302.7 16.3 %copy.13 = bf16[1152,5120]{1,0:T(8,128)(2,1)} copy(bf16[1152,5120]{0,1:T(8,128)(2,1)} %bitcast.12) | data formatting | bytes 23592960
  (4 shorter events, 0.0 us)
Async XLA Ops:
  7.2 99.1 %all-gather.9.cloned.1.call-start = ((), (), s32[]{:S(2)}) async-start(), calls=%async_computation.5 | async-start | bytes 4423680 | tf_op jit(solution)/shard_map/all_gather | solution.py:29
  65.2 45.1 %copy-start = (s32[1024]{0:T(1024)S(1)}, s32[1024]{0:T(1024)}, u32[]{:S(2)}) copy-start(s32[1024]{0:T(1024)} %param.5) | copy-start | bytes 12292
  65.3 126.8 %all-gather.5.cloned.1.call-start = ((), (), s32[]{:S(2)}) async-start(), calls=%async_computation.3 | async-start | bytes 11141120 | tf_op jit(solution)/shard_map/all_gather | solution.py:40
  66.0 236.7 %all-gather.7.cloned.1.call-start = ((), (), s32[]{:S(2)}) async-start(), calls=%async_computation.4 | async-start | bytes 14745600 | tf_op jit(solution)/shard_map/all_gather | solution.py:29
Sparse Core Ops, SparseCore 0:
  65.4 40.8 all-gather.8
  108.8 83.2 all-gather.4
  193.7 108.8 all-gather.6
where the time goes:
time: 326 us; the launch traced here: 325 us
  waiting for transfers between devices  199 us (61%)
  blocking collectives  66 us (20%)
  local copies, waits for them, and re-layouts  22.8 us (7%)
  matrix products  19.5 us (6%)
  between operations  13.8 us (4%)
  other arithmetic  3.87 us (1%)
    all_gather x2, waiting for transfers between devices, whole_of(): nearer = lax.all_gather(shard, axes[-1], axis=dim, tiled=True)  117 us
    all_gather x1, waiting for transfers between devices, on_device(): lax.all_gather(hidden, 'vocab', axis=0, tiled=True)  81.7 us
    all_to_all x1, blocking collectives, on_device(): lax.all_to_all(lax.all_to_all(new_weight, DP, split_axis=1, concat_axis=0...  31 us
    all_to_all x1, blocking collectives, on_device(): lax.all_to_all(new_weight, DP, split_axis=1, concat_axis=0, tiled=True)  24.7 us
    dot_general x1, matrix products, on_device(): lax.dot_general(lax.all_gather(hidden, 'vocab', axis=0, tiled=True), old_...  19.5 us
    unnamed x4, local copies, waits for them, and re-layouts  16.3 us
    all_to_all x1, blocking collectives, sent_together(): lax.all_to_all(both, axis, split_axis=split_dim, concat_axis=concat_dim,...  10.4 us
  transfers between devices with their start and end apart: 3, of which 3 were waited for; matrix products, arithmetic and copies ran while one was open for 8% of the time, Pallas kernels for 0%

commit v1 on v0

v1 whole, which is shorter than its diff:
```python
import functools

import jax
import jax.numpy as jnp
from jax import lax
from jax.experimental import pallas as pl
from jax.experimental.pallas import tpu as pltpu
from jax.sharding import Mesh
from jax.sharding import PartitionSpec as P

AXES = ("x", "ylo", "z", "yhi", "c")
DP = ("x", "ylo")
VOCAB = ("z", "yhi", "c")
MESH = pl.DeviceIdType.MESH

CHUNKS = 36
HALVES = 3
BLOCK = 128
LAG_SWAP, LAG_X, LAG_FAR, LAG_Z, LAG_RELAY, LAG_Y, LAG_X2 = 1, 2, 4, 6, 8, 10, 12
STEPS = CHUNKS + LAG_X2
STEP_NEAR, STEP_FAR, STEP_OWN, STEP_OTHER = 7, 13, 18, 39
STEP_HIDDEN, EVERY, STEP_ARRIVED = 1, 2, 11
PIECES = 4
VOCAB_TILES = 3
LANES = 128
WRITES = 8

(S_HALF, S_SWAP, S_X, S_FAR, S_Z, S_RELAY, S_Y, S_X2, S_HZ, S_HFAR, S_HC, S_HY, S_HC2,
 S_TOK, S_STAT, N_SEND) = range(16)
(R_X2, R_HZ, R_HFAR, R_HC, R_HC2, R_TOK, R_STAT, R_OWN, R_OWN_TOK, R_WEIGHT, N_ONE) = range(11)


def kernel(hid, tok, old, new, out, logprob, halves, merged, near, relay, rows_all, weight, logits,
           stats, got, tokens, send, one, half_in, swap_in, x_in, far_in, relay_in, z_in, y_in, hy_in):
    x, ylo, z, yhi, c = (lax.axis_index(a) for a in AXES)
    nx, nz = lax.axis_size("x"), lax.axis_size("z")
    up_x, down_x = lax.rem(x + 1, nx), lax.rem(x + nx - 1, nx)
    up_z, down_z = lax.rem(z + 1, nz), lax.rem(z + nz - 1, nz)
    far_z = lax.rem(z + 2, nz)
    other = 1 - c
    swaps = ylo != yhi
    flip = {"yhi": 1 - yhi, "ylo": 1 - ylo}
    my_rows, cols = merged.shape
    size = my_rows // CHUNKS
    part = my_rows // HALVES
    own = hid.shape[0]
    sub = own // PIECES

    def remote(src, dst, s, recv, device):
        return pltpu.make_async_remote_copy(
            src_ref=src, dst_ref=dst, send_sem=send.at[s], recv_sem=recv,
            device_id=device, device_id_type=MESH)

    def landed(ref, sem):
        pltpu.make_async_copy(ref, ref, sem).wait()

    def at(k):
        return pl.ds(pl.multiple_of(k * size, size), size)

    def col(zs, low):
        return pl.ds(pl.multiple_of((2 * zs + low) * cols, LANES), cols)

    barrier = pltpu.get_barrier_semaphore()
    peers = [{"x": up_x}, {"x": down_x}, {"ylo": 1 - ylo}]
    for dz in range(4):
        for same in (True, False):
            for dc in range(2):
                if dz == 0 and same and dc == 0:
                    continue
                peer = {"z": lax.rem(z + dz, nz), "c": lax.rem(c + dc, 2)}
                peers.append(peer if same else {**peer, **flip})
    for peer in peers:
        pl.semaphore_signal(barrier, inc=1, device_id=peer, device_id_type=MESH)
    pl.semaphore_wait(barrier, len(peers))

    for q in range(HALVES):
        here = pl.ds(pl.multiple_of(c * my_rows + q * part, part), part)
        there = pl.ds(pl.multiple_of(other * my_rows + q * part, part), part)
        mine = halves.at[c, :, pl.ds(q * part, part)]
        remote(new.at[:, there], mine, S_HALF, half_in.at[q], {"c": other}).start()
        pltpu.make_async_copy(new.at[:, here], mine, half_in.at[q]).start()
    own_block = rows_all.at[0, z, c]
    for device in (up_z, down_z):
        remote(hid, own_block, S_HZ, one.at[R_HZ], {"z": device}).start()
    pltpu.make_async_copy(hid, own_block, one.at[R_OWN]).start()
    pltpu.make_async_copy(tok, tokens.at[0], one.at[R_OWN_TOK]).start()
    remote(tok, tokens.at[1], S_TOK, one.at[R_TOK], flip).start()
    load_weight = pltpu.make_async_copy(old, weight, one.at[R_WEIGHT])
    load_weight.start()
    landed(rows_all.at[0, z, c], one.at[R_OWN])
    landed(tokens.at[0], one.at[R_OWN_TOK])
    remote(own_block, own_block, S_HC, one.at[R_HC], {"c": other}).start()

    def merge(k):
        @pl.when(lax.rem(k, CHUNKS // HALVES) == 0)
        def _():
            q = k // (CHUNKS // HALVES)
            landed(halves.at[:, :, pl.ds(pl.multiple_of(q * part, part), part)], half_in.at[q])

        @pl.when(lax.rem(k, BLOCK // size) == 0)
        def _():
            ids = pl.ds(pl.multiple_of(k * size, BLOCK), BLOCK)
            both = jnp.concatenate([halves[0, :, ids], halves[1, :, ids]], axis=0)
            merged[ids, :] = both.T

    def swap(k):
        mine = near.at[x, at(k)]

        @pl.when(swaps)
        def _():
            remote(merged.at[at(k)], mine, S_SWAP, swap_in.at[k], flip).start()

        @pl.when(jnp.logical_not(swaps))
        def _():
            pltpu.make_async_copy(merged.at[at(k)], mine, swap_in.at[k]).start()

    def along_x(k):
        mine = near.at[x, at(k)]
        landed(mine, swap_in.at[k])
        remote(mine, mine, S_X, x_in.at[k], {"x": up_x}).start()
        remote(mine, mine, S_X, x_in.at[k], {"x": down_x}).start()

    def direction(k):
        return 1 - 2 * lax.rem(k, 2)

    def far_x(k):
        landed(near.at[pl.ds(0, 2), at(k)], x_in.at[k])
        d = direction(k)
        piece = near.at[lax.rem(x + nx - d, nx), at(k)]
        remote(piece, piece, S_FAR, far_in.at[k], {"x": lax.rem(x + nx + d, nx)}).start()

    def along_z(k):
        landed(near.at[0, at(k)], far_in.at[k])
        d = direction(k)
        target = out.at[at(k), col(z, ylo)]
        remote(near.at[far_z, at(k)], relay.at[at(k)], S_Z, relay_in.at[k],
               {"z": lax.rem(z + nz + d, nz)}).start()
        remote(near.at[up_z, at(k)], target, S_Z, z_in.at[k], {"z": up_z}).start()
        remote(near.at[down_z, at(k)], target, S_Z, z_in.at[k], {"z": down_z}).start()
        pltpu.make_async_copy(near.at[z, at(k)], target, z_in.at[k]).start()

    def relay_z(k):
        landed(relay.at[at(k)], relay_in.at[k])
        d = direction(k)
        source = lax.rem(z + nz - d, nz)
        remote(relay.at[at(k)], out.at[at(k), col(source, ylo)], S_RELAY, z_in.at[k],
               {"z": lax.rem(z + nz + d, nz)}).start()

    def along_y(k):
        landed(out.at[at(k), pl.ds(0, 4 * cols)], z_in.at[k])
        for add in (0, 2):
            piece = out.at[at(k), col(lax.rem(x, 2) + add, ylo)]
            remote(piece, piece, S_Y, y_in.at[k], {"ylo": 1 - ylo}).start()

    def along_x2(k):
        landed(out.at[at(k), pl.ds(0, 2 * cols)], y_in.at[k])
        for add, device in ((0, up_x), (2, down_x)):
            piece = out.at[at(k), col(lax.rem(x, 2) + add, 1 - ylo)]
            remote(piece, piece, S_X2, one.at[R_X2], {"x": device}).start()

    def near_hidden():
        landed(rows_all.at[0, pl.ds(0, 2), 0], one.at[R_HZ])
        for source, device, first in ((down_z, up_z, 0), (up_z, down_z, own // 2)):
            piece = rows_all.at[0, source, c, pl.ds(first, own // 2)]
            remote(piece, piece, S_HFAR, one.at[R_HFAR], {"z": device}).start()
        for source in (down_z, up_z):
            block = rows_all.at[0, source, c]
            remote(block, block, S_HC, one.at[R_HC], {"c": other}).start()

    def far_hidden():
        landed(rows_all.at[0, 0, 0], one.at[R_HFAR])
        block = rows_all.at[0, far_z, c]
        remote(block, block, S_HC, one.at[R_HC], {"c": other}).start()

    def offset_of(b):
        return lax.rem(b * (7 - b) // 2, 4)

    def hidden_y(j):
        b = j // PIECES
        source = lax.rem(z + offset_of(b), nz)
        lines = pl.ds(pl.multiple_of(lax.rem(j, PIECES) * sub, sub), sub)
        remote(rows_all.at[0, source, c, lines], rows_all.at[1, source, c, lines], S_HY,
               hy_in.at[b], flip).start()

    def hidden_y_in(b):
        block = rows_all.at[1, lax.rem(z + offset_of(b), nz), c]
        landed(block, hy_in.at[b])
        remote(block, block, S_HC2, one.at[R_HC2], {"c": other}).start()

    tile = weight.shape[0] // VOCAB_TILES
    wide = 4 * own
    first_id = ((z * 2 + yhi) * 2 + c) * weight.shape[0]

    def dot_step(nb, m):
        lines = pl.ds(pl.multiple_of(m * tile, tile), tile)
        rows = rows_all[nb // 2, pl.ds(lax.rem(nb, 2) * 2, 2)].reshape(wide, hid.shape[1])
        logits[lines, :] = lax.dot_general(
            weight[lines, :], rows, (((1,), (1,)), ((), ())),
            preferred_element_type=jnp.float32)

    def stat_step(nb):
        side = nb // 2
        high = yhi + side - 2 * yhi * side
        for i in range(2):
            zs = lax.rem(nb, 2) * 2 + i
            values = logits[:, i * LANES:(i + 1) * LANES]
            top = jnp.max(values, axis=0, keepdims=True)
            total = jnp.sum(jnp.exp(values - top), axis=0, keepdims=True)
            wanted = tokens[side, pl.ds(zs * 2 + high, 1), :] - first_id
            ids = lax.broadcasted_iota(jnp.int32, values.shape, 0)
            hit = jnp.sum(jnp.where(ids == wanted, values, 0.0), axis=0, keepdims=True)
            slot = side * 4 + zs
            stats[slot, 0:1, :] = top
            stats[slot, 1:2, :] = total
            stats[slot, 2:3, :] = hit

    def compute(first, e):
        nb, m = first + e // (VOCAB_TILES + 1), lax.rem(e, VOCAB_TILES + 1)

        @pl.when(m < VOCAB_TILES)
        def _():
            dot_step(nb, m)

        @pl.when(m == VOCAB_TILES)
        def _():
            stat_step(nb)

    events = 2 * (VOCAB_TILES + 1)

    def step(t, carry):
        stages = ((LAG_X2, along_x2), (LAG_Y, along_y), (LAG_RELAY, relay_z), (LAG_Z, along_z),
                  (LAG_FAR, far_x), (LAG_X, along_x), (LAG_SWAP, swap), (0, merge))
        for lag, stage in stages:
            k = t - lag

            @pl.when(jnp.logical_and(k >= 0, k < CHUNKS))
            def _(stage=stage, k=k):
                stage(k)

        pl.when(t == STEP_NEAR)(near_hidden)
        pl.when(t == STEP_FAR)(far_hidden)

        piece = t - STEP_HIDDEN

        @pl.when((piece >= 0) & (lax.rem(piece, EVERY) == 0) & (piece < 4 * PIECES * EVERY))
        def _():
            hidden_y(piece // EVERY)

        block = t - STEP_ARRIVED
        period = PIECES * EVERY

        @pl.when((block >= 0) & (lax.rem(block, period) == 0) & (block < 4 * period))
        def _():
            hidden_y_in(block // period)

        @pl.when(t == STEP_OWN)
        def _():
            landed(rows_all.at[0, :, 0], one.at[R_HC])
            landed(weight, one.at[R_WEIGHT])
            landed(tokens.at[1], one.at[R_TOK])

        @pl.when(t == STEP_OTHER)
        def _():
            landed(rows_all.at[1, :, 0], one.at[R_HC2])

        @pl.when((t >= STEP_OWN) & (t < STEP_OWN + events))
        def _():
            compute(0, t - STEP_OWN)

        @pl.when((t >= STEP_OTHER) & (t < STEP_OTHER + events))
        def _():
            compute(2, t - STEP_OTHER)
        return carry

    lax.fori_loop(0, STEPS, step, 0)

    for side in range(2):
        for dz in range(4):
            for dc in range(2):
                zs = lax.rem(z + dz, nz)
                src = stats.at[side * 4 + zs]
                dst = got.at[(side * 4 + z) * 2 + c]
                if side == 0 and dz == 0 and dc == 0:
                    pltpu.make_async_copy(src, dst, one.at[R_STAT]).start()
                else:
                    peer = {"z": zs, "c": lax.rem(c + dc, 2)}
                    remote(src, dst, S_STAT, one.at[R_STAT], peer if side == 0 else {**peer, **flip}).start()
    landed(got, one.at[R_STAT])
    tops = got[:, 0, :]
    top = jnp.max(tops, axis=0, keepdims=True)
    total = jnp.sum(got[:, 1, :] * jnp.exp(tops - top), axis=0, keepdims=True)
    target = jnp.sum(got[:, 2, :], axis=0, keepdims=True)
    logprob[...] = target - top - jnp.log(total)

    landed(out.at[:, pl.ds(0, 2 * cols)], one.at[R_X2])
    landed(halves.at[0], send.at[S_HALF])
    pl.when(swaps)(lambda: landed(merged, send.at[S_SWAP]))
    landed(near.at[pl.ds(0, 2)], send.at[S_X])
    landed(near.at[0], send.at[S_FAR])
    landed(near.at[pl.ds(0, 3)], send.at[S_Z])
    landed(relay, send.at[S_RELAY])
    landed(near.at[pl.ds(0, 2)], send.at[S_Y])
    landed(near.at[pl.ds(0, 2)], send.at[S_X2])
    landed(rows_all.at[0, pl.ds(0, 2), 0], send.at[S_HZ])
    landed(rows_all.at[0, 0, 0], send.at[S_HFAR])
    landed(rows_all.at[0, :, 0], send.at[S_HC])
    landed(rows_all.at[0, :, 0], send.at[S_HY])
    landed(rows_all.at[0, :, 0], send.at[S_HC2])
    landed(tokens.at[0], send.at[S_TOK])
    landed(got.at[pl.ds(0, 15)], send.at[S_STAT])


def write_out(held, both, out, both_out, sem):
    part = held.shape[0] // WRITES
    copies = [pltpu.make_async_copy(held.at[pl.ds(i * part, part)], out.at[pl.ds(i * part, part)], sem.at[i])
              for i in range(WRITES)]
    for copy in copies:
        copy.start()
    both_out[...] = both[...]
    for copy in copies:
        copy.wait()


def on_device(hidden, tokens, old_weight, new_weight):
    own, width = hidden.shape
    vocab_rows = old_weight.shape[0]
    cols = 2 * new_weight.shape[1]
    sems = pltpu.SemaphoreType.DMA
    engine_weight, both = pl.pallas_call(
        kernel,
        out_shape=(
            pltpu.VMEM((vocab_rows, width), jnp.bfloat16),
            jax.ShapeDtypeStruct((1, LANES), jnp.float32),
        ),
        in_specs=[pl.BlockSpec(memory_space=pl.ANY)] * 4,
        out_specs=(pl.BlockSpec(memory_space=pltpu.VMEM), pl.BlockSpec(memory_space=pltpu.VMEM)),
        scratch_shapes=[
            pltpu.VMEM((2, cols // 2, vocab_rows), jnp.bfloat16),
            pltpu.VMEM((vocab_rows, cols), jnp.bfloat16),
            pltpu.VMEM((4, vocab_rows, cols), jnp.bfloat16),
            pltpu.VMEM((vocab_rows, cols), jnp.bfloat16),
            pltpu.VMEM((2, 4, 2, own, width), jnp.bfloat16),
            pltpu.VMEM((vocab_rows, width), jnp.bfloat16),
            pltpu.VMEM((vocab_rows, 4 * own), jnp.float32),
            pltpu.VMEM((8, 8, LANES), jnp.float32),
            pltpu.VMEM((16, 8, LANES), jnp.float32),
            pltpu.VMEM((2, 8, LANES), jnp.int32),
            sems((N_SEND,)),
            sems((N_ONE,)),
            sems((HALVES,)),
            sems((CHUNKS,)),
            sems((CHUNKS,)),
            sems((CHUNKS,)),
            sems((CHUNKS,)),
            sems((CHUNKS,)),
            sems((CHUNKS,)),
            sems((4,)),
        ],
        compiler_params=pltpu.CompilerParams(
            collective_id=0, has_side_effects=True, vmem_limit_bytes=40 * 2**20
        ),
    )(hidden, tokens.reshape(8, LANES), old_weight, new_weight.T)
    engine_weight, both = pl.pallas_call(
        write_out,
        out_shape=(
            jax.ShapeDtypeStruct((vocab_rows, width), jnp.bfloat16),
            jax.ShapeDtypeStruct((1, LANES), jnp.float32),
        ),
        in_specs=[pl.BlockSpec(memory_space=pl.ANY), pl.BlockSpec(memory_space=pltpu.VMEM)],
        out_specs=(pl.BlockSpec(memory_space=pl.ANY), pl.BlockSpec(memory_space=pltpu.VMEM)),
        scratch_shapes=[sems((WRITES,))],
        compiler_params=pltpu.CompilerParams(vmem_limit_bytes=2**20),
    )(engine_weight, both)
    logprob = lax.dynamic_slice(both, (0, lax.axis_index("c") * own), (1, own))
    return logprob.reshape(own), engine_weight


def solution(mesh):
    finer = Mesh(mesh.devices.reshape(4, 2, 4, 2, 2), AXES)
    return jax.shard_map(
        on_device,
        mesh=finer,
        in_specs=(P(DP + VOCAB, None), P(DP), P(VOCAB, None), P(DP, VOCAB)),
        out_specs=(P(DP + VOCAB), P(VOCAB, None)),
        check_vma=False,
    )
```

time: 326 us -> 166 us (0.51)
  waiting for transfers between devices: 199 us -> 0 us
  Pallas kernels: 0 us -> 161 us
  blocking collectives: 66 us -> 0 us
  matrix products: 19.5 us -> 0 us
  local copies, waits for them, and re-layouts: 22.8 us -> 3.72 us
  between operations: 13.8 us -> 0.66 us
  other arithmetic: 3.87 us -> 0 us
    all_gather x3 -> x0, waiting for transfers between devices: 199 us -> none  [the longest x2 117 us: whole_of(): nearer = lax.all_gather(shard, axes[-1], axis=dim, tiled=True)]
    pallas_call x0 -> x2, Pallas kernels: none -> 161 us  [the longest x1 157 us: on_device(): pl.pallas_call(kernel, out_shape=(pltpu.VMEM((vocab_rows, width), jnp.bfl...]
    all_to_all x3 -> x0, blocking collectives: 66 us -> none  [the longest x1 31 us: on_device(): lax.all_to_all(lax.all_to_all(new_weight, DP, split_axis=1, concat_axis=0...]
    dot_general x1 -> x0, matrix products: 19.5 us -> none  [on_device(): lax.dot_general(lax.all_gather(hidden, 'vocab', axis=0, tiled=True), old_...]
    unnamed x4 -> x6, local copies, waits for them, and re-layouts: 16.3 us -> 3.14 us
    all_gather x1 -> x0, local copies, waits for them, and re-layouts: 3.99 us -> none  [whole_of(): nearer = lax.all_gather(shard, axes[-1], axis=dim, tiled=True)]
  transfers between devices with their start and end apart: 3 -> 0, of which waited for: 3 -> 0; matrix products, arithmetic and copies ran while one was open for 8% -> 0% of each run, Pallas kernels for 0% -> 0%
where the time goes in v1:
time: 166 us; the launch traced here: 165 us
  Pallas kernels  161 us (97%)
  local copies, waits for them, and re-layouts  3.72 us (2%)
    pallas_call x1, Pallas kernels, on_device(): pl.pallas_call(kernel, out_shape=(pltpu.VMEM((vocab_rows, width), jnp.bfl...  157 us
    pallas_call x1, Pallas kernels, on_device(): pl.pallas_call(write_out, out_shape=(jax.ShapeDtypeStruct((vocab_rows, wi...  4.41 us

profile of v1, /device:TPU:1, one launch (start us, length us, event | category | flops | bytes accessed | tf_op | source)
XLA Modules:
  0.0 165.4 jit_solution(12808662790416252979)
XLA Ops:
  0.6 0.0 copy-start
  0.6 1.4 copy-done
  2.0 0.0 copy-start.1
  2.0 1.1 copy-done.1
  3.1 0.0 copy-start.2
  3.1 0.7 copy-done.2
  3.8 156.6 %shard_map.59 = (bf16[1152,5120]{1,0:T(8,128)(2,1)S(1)}, f32[1,128]{1,0:T(1,128)S(1)}) custom-call(bf16[64,5120]{1,0:T(8,128)(2,1)S(1)} %copy-done.1, s32[8,128]{1,0:T(8,128)S(1)} %bitcast.5, bf16[1152,5120]{1,0:T(8,128)(2,1)} %old.1, bf16[320,2304]{1,0:T(8,128)(2,1)S(1)} %bitcast.4), custom_call_target="tpu_custom_call" | custom-call | tf_op jit(solution)/shard_map/pallas_call | solution.py:329
  160.4 4.4 %shard_map.60 = (bf16[1152,5120]{1,0:T(8,128)(2,1)}, f32[1,128]{1,0:T(1,128)S(1)}) custom-call(bf16[1152,5120]{1,0:T(8,128)(2,1)S(1)} %get-tuple-element.6.held, f32[1,128]{1,0:T(1,128)S(1)} %get-tuple-element.7.both), custom_call_target="tpu_custom_call" | custom-call | tf_op jit(solution)/shard_map/pallas_call | solution.py:363
  164.9 0.6 dynamic-slice_bitcast_fusion
Async XLA Ops:
  0.6 1.4 copy-start
  2.0 1.1 copy-start.1
  3.1 0.7 copy-start.2

commit v2 on v1

--- a/solution.py
+++ b/solution.py
@@ -13,25 +13,26 @@
 VOCAB = ("z", "yhi", "c")
 MESH = pl.DeviceIdType.MESH
 
-CHUNKS = 36
+CHUNKS = 18
 HALVES = 3
 BLOCK = 128
-LAG_SWAP, LAG_X, LAG_FAR, LAG_Z, LAG_RELAY, LAG_Y, LAG_X2 = 1, 2, 4, 6, 8, 10, 12
-STEPS = CHUNKS + LAG_X2
-STEP_NEAR, STEP_FAR, STEP_OWN, STEP_OTHER = 7, 13, 18, 39
-STEP_HIDDEN, EVERY, STEP_ARRIVED = 1, 2, 11
+LAG_SWAP, LAG_X, LAG_FAR, LAG_Z, LAG_RELAY, LAG_Y, LAG_X2 = 1, 8, 12, 17, 19, 21, 27
+STEP_NEAR, STEP_FAR, STEP_OWN, STEP_OTHER = 12, 21, 22, 31
+STEP_HIDDEN, EVERY, STEP_ARRIVED = 21, 1, 29
 PIECES = 4
+PERIOD = PIECES * EVERY
 VOCAB_TILES = 3
+STEPS = max(CHUNKS + LAG_X2, STEP_OTHER + 3 * PERIOD + VOCAB_TILES + 1)
 LANES = 128
 WRITES = 8
 
 (S_HALF, S_SWAP, S_X, S_FAR, S_Z, S_RELAY, S_Y, S_X2, S_HZ, S_HFAR, S_HC, S_HY, S_HC2,
  S_TOK, S_STAT, N_SEND) = range(16)
-(R_X2, R_HZ, R_HFAR, R_HC, R_HC2, R_TOK, R_STAT, R_OWN, R_OWN_TOK, R_WEIGHT, N_ONE) = range(11)
+(R_X2, R_HZ, R_HFAR, R_HC,  R_TOK, R_STAT, R_OWN, R_OWN_TOK, R_WEIGHT, N_ONE) = range(10)
 
 
 def kernel(hid, tok, old, new, out, logprob, halves, merged, near, relay, rows_all, weight, logits,
-           stats, got, tokens, send, one, half_in, swap_in, x_in, far_in, relay_in, z_in, y_in, hy_in):
+           stats, got, tokens, send, one, half_in, swap_in, x_in, far_in, relay_in, z_in, y_in, hy_in, hc2_in):
     x, ylo, z, yhi, c = (lax.axis_index(a) for a in AXES)
     nx, nz = lax.axis_size("x"), lax.axis_size("z")
     up_x, down_x = lax.rem(x + 1, nx), lax.rem(x + nx - 1, nx)
@@ -185,45 +186,57 @@
     def hidden_y_in(b):
         block = rows_all.at[1, lax.rem(z + offset_of(b), nz), c]
         landed(block, hy_in.at[b])
-        remote(block, block, S_HC2, one.at[R_HC2], {"c": other}).start()
+        remote(block, block, S_HC2, hc2_in.at[b], {"c": other}).start()
 
     tile = weight.shape[0] // VOCAB_TILES
-    wide = 4 * own
     first_id = ((z * 2 + yhi) * 2 + c) * weight.shape[0]
 
-    def dot_step(nb, m):
+    def dot_step(m, rows, lanes):
         lines = pl.ds(pl.multiple_of(m * tile, tile), tile)
-        rows = rows_all[nb // 2, pl.ds(lax.rem(nb, 2) * 2, 2)].reshape(wide, hid.shape[1])
-        logits[lines, :] = lax.dot_general(
-            weight[lines, :], rows, (((1,), (1,)), ((), ())),
+        logits[lines, 0:lanes] = lax.dot_general(
+            weight[lines, :], rows.reshape(lanes, hid.shape[1]), (((1,), (1,)), ((), ())),
             preferred_element_type=jnp.float32)
 
-    def stat_step(nb):
-        side = nb // 2
-        high = yhi + side - 2 * yhi * side
-        for i in range(2):
-            zs = lax.rem(nb, 2) * 2 + i
-            values = logits[:, i * LANES:(i + 1) * LANES]
-            top = jnp.max(values, axis=0, keepdims=True)
-            total = jnp.sum(jnp.exp(values - top), axis=0, keepdims=True)
-            wanted = tokens[side, pl.ds(zs * 2 + high, 1), :] - first_id
-            ids = lax.broadcasted_iota(jnp.int32, values.shape, 0)
-            hit = jnp.sum(jnp.where(ids == wanted, values, 0.0), axis=0, keepdims=True)
-            slot = side * 4 + zs
-            stats[slot, 0:1, :] = top
-            stats[slot, 1:2, :] = total
-            stats[slot, 2:3, :] = hit
-
-    def compute(first, e):
-        nb, m = first + e // (VOCAB_TILES + 1), lax.rem(e, VOCAB_TILES + 1)
+    def stat_step(side, zs, first):
+        high = 1 - yhi if side else yhi
+        values = logits[:, first:first + LANES]
+        top = jnp.max(values, axis=0, keepdims=True)
+        total = jnp.sum(jnp.exp(values - top), axis=0, keepdims=True)
+        wanted = tokens[side, pl.ds(zs * 2 + high, 1), :] - first_id
+        ids = lax.broadcasted_iota(jnp.int32, values.shape, 0)
+        hit = jnp.sum(jnp.where(ids == wanted, values, 0.0), axis=0, keepdims=True)
+        slot = side * 4 + zs
+        stats[slot, 0:1, :] = top
+        stats[slot, 1:2, :] = total
+        stats[slot, 2:3, :] = hit
+
+    def compute_own(e):
+        pair, m = e // (VOCAB_TILES + 1), lax.rem(e, VOCAB_TILES + 1)
 
         @pl.when(m < VOCAB_TILES)
         def _():
-            dot_step(nb, m)
+            dot_step(m, rows_all[0, pl.ds(pair * 2, 2)], 2 * LANES)
 
         @pl.when(m == VOCAB_TILES)
         def _():
-            stat_step(nb)
+            for i in range(2):
+                stat_step(0, pair * 2 + i, i * LANES)
+
+    def compute_other(e):
+        b, m = e // PERIOD, lax.rem(e, PERIOD)
+        zs = lax.rem(z + offset_of(b), nz)
+
+        @pl.when(m == 0)
+        def _():
+            landed(rows_all.at[1, 0, 0], hc2_in.at[b])
+
+        @pl.when(m < VOCAB_TILES)
+        def _():
+            dot_step(m, rows_all[1, zs], LANES)
+
+        @pl.when(m == VOCAB_TILES)
+        def _():
+            stat_step(1, zs, 0)
 
     events = 2 * (VOCAB_TILES + 1)
 
@@ -247,11 +260,10 @@
             hidden_y(piece // EVERY)
 
         block = t - STEP_ARRIVED
-        period = PIECES * EVERY
-
-        @pl.when((block >= 0) & (lax.rem(block, period) == 0) & (block < 4 * period))
-        def _():
-            hidden_y_in(block // period)
+
+        @pl.when((block >= 0) & (lax.rem(block, PERIOD) == 0) & (block < 4 * PERIOD))
+        def _():
+            hidden_y_in(block // PERIOD)
 
         @pl.when(t == STEP_OWN)
         def _():
@@ -259,17 +271,13 @@
             landed(weight, one.at[R_WEIGHT])
             landed(tokens.at[1], one.at[R_TOK])
 
-        @pl.when(t == STEP_OTHER)
-        def _():
-            landed(rows_all.at[1, :, 0], one.at[R_HC2])
-
         @pl.when((t >= STEP_OWN) & (t < STEP_OWN + events))
         def _():
-            compute(0, t - STEP_OWN)
-
-        @pl.when((t >= STEP_OTHER) & (t < STEP_OTHER + events))
-        def _():
-            compute(2, t - STEP_OTHER)
+            compute_own(t - STEP_OWN)
+
+        @pl.when((t >= STEP_OTHER) & (t < STEP_OTHER + 4 * PERIOD))
+        def _():
+            compute_other(t - STEP_OTHER)
         return carry
 
     lax.fori_loop(0, STEPS, step, 0)
@@ -332,7 +340,7 @@
             pltpu.VMEM((vocab_rows, width), jnp.bfloat16),
             jax.ShapeDtypeStruct((1, LANES), jnp.float32),
         ),
-        in_specs=[pl.BlockSpec(memory_space=pl.ANY)] * 4,
+        in_specs=[pl.BlockSpec(memory_space=pltpu.HBM)] * 4,
         out_specs=(pl.BlockSpec(memory_space=pltpu.VMEM), pl.BlockSpec(memory_space=pltpu.VMEM)),
         scratch_shapes=[
             pltpu.VMEM((2, cols // 2, vocab_rows), jnp.bfloat16),
@@ -355,11 +363,12 @@
             sems((CHUNKS,)),
             sems((CHUNKS,)),
             sems((4,)),
+            sems((4,)),
         ],
         compiler_params=pltpu.CompilerParams(
             collective_id=0, has_side_effects=True, vmem_limit_bytes=40 * 2**20
         ),
-    )(hidden, tokens.reshape(8, LANES), old_weight, new_weight.T)
+    )(*(pltpu.with_memory_space_constraint(a, pltpu.HBM) for a in (hidden, tokens.reshape(8, LANES), old_weight, new_weight.T)))
     engine_weight, both = pl.pallas_call(
         write_out,
         out_shape=(

time: 166 us -> 120 us (0.72)
  Pallas kernels: 161 us -> 118 us
  local copies, waits for them, and re-layouts: 3.72 us -> 0.59 us
    pallas_call x1, Pallas kernels: 157 us -> 114 us  [on_device(): pl.pallas_call(kernel, out_shape=(pltpu.VMEM((vocab_rows, width), jnp.bfl...]
    unnamed x6 -> x0, local copies, waits for them, and re-layouts: 3.14 us -> none
where the time goes in v2:
time: 120 us; the launch traced here: 119 us
  Pallas kernels  118 us (98%)
    pallas_call x1, Pallas kernels, on_device(): pl.pallas_call(kernel, out_shape=(pltpu.VMEM((vocab_rows, width), jnp.bfl...  114 us
    pallas_call x1, Pallas kernels, on_device(): pl.pallas_call(write_out, out_shape=(jax.ShapeDtypeStruct((vocab_rows, wi...  4.41 us

profile of v2, /device:TPU:1, one launch (start us, length us, event | category | flops | bytes accessed | tf_op | source)
XLA Modules:
  0.0 119.5 jit_solution(2869669454158011335)
XLA Ops:
  0.6 113.8 %shard_map.59 = (bf16[1152,5120]{1,0:T(8,128)(2,1)S(1)}, f32[1,128]{1,0:T(1,128)S(1)}) custom-call(bf16[64,5120]{1,0:T(8,128)(2,1)} %hid.1, s32[8,128]{1,0:T(8,128)} %bitcast.5, bf16[1152,5120]{1,0:T(8,128)(2,1)} %old.1, bf16[320,2304]{1,0:T(8,128)(2,1)} %bitcast.4), custom_call_target="tpu_custom_call" | custom-call | tf_op jit(solution)/shard_map/pallas_call | solution.py:337
  114.5 4.4 %shard_map.60 = (bf16[1152,5120]{1,0:T(8,128)(2,1)}, f32[1,128]{1,0:T(1,128)S(1)}) custom-call(bf16[1152,5120]{1,0:T(8,128)(2,1)S(1)} %get-tuple-element.6.held, f32[1,128]{1,0:T(1,128)S(1)} %get-tuple-element.7.both), custom_call_target="tpu_custom_call" | custom-call | tf_op jit(solution)/shard_map/pallas_call | solution.py:372
  118.9 0.6 dynamic-slice_bitcast_fusion

commit v3 on v2

--- a/solution.py
+++ b/solution.py
@@ -16,9 +16,11 @@
 CHUNKS = 18
 HALVES = 3
 BLOCK = 128
-LAG_SWAP, LAG_X, LAG_FAR, LAG_Z, LAG_RELAY, LAG_Y, LAG_X2 = 1, 8, 12, 17, 19, 21, 27
-STEP_NEAR, STEP_FAR, STEP_OWN, STEP_OTHER = 12, 21, 22, 31
-STEP_HIDDEN, EVERY, STEP_ARRIVED = 21, 1, 29
+LAG_SWAP, LAG_X, LAG_FAR, LAG_Z, LAG_RELAY, LAG_Y, LAG_X2 = 2, 10, 13, 15, 17, 19, 24
+ORDER = ("merge", "far_x", "x2", "y", "swap", "x", "relay", "z")
+STEP_NEAR, STEP_ON, STEP_ON2, STEP_FAR, STEP_OWN, STEP_OTHER = 11, 11, 12, 16, 17, 25
+STEP_HIDDEN, EVERY, STEP_ARRIVED = 12, 1, 24
+EARLY = 2
 PIECES = 4
 PERIOD = PIECES * EVERY
 VOCAB_TILES = 3
@@ -63,13 +65,7 @@
 
     barrier = pltpu.get_barrier_semaphore()
     peers = [{"x": up_x}, {"x": down_x}, {"ylo": 1 - ylo}]
-    for dz in range(4):
-        for same in (True, False):
-            for dc in range(2):
-                if dz == 0 and same and dc == 0:
-                    continue
-                peer = {"z": lax.rem(z + dz, nz), "c": lax.rem(c + dc, 2)}
-                peers.append(peer if same else {**peer, **flip})
+    peers += [{"z": up_z}, {"z": down_z}, {"c": other}, flip]
     for peer in peers:
         pl.semaphore_signal(barrier, inc=1, device_id=peer, device_id_type=MESH)
     pl.semaphore_wait(barrier, len(peers))
@@ -81,6 +77,9 @@
         remote(new.at[:, there], mine, S_HALF, half_in.at[q], {"c": other}).start()
         pltpu.make_async_copy(new.at[:, here], mine, half_in.at[q]).start()
     own_block = rows_all.at[0, z, c]
+    for j in range(EARLY):
+        lines = pl.ds(j * sub, sub)
+        remote(hid.at[lines], rows_all.at[1, z, c, lines], S_HY, hy_in.at[0], flip).start()
     for device in (up_z, down_z):
         remote(hid, own_block, S_HZ, one.at[R_HZ], {"z": device}).start()
     pltpu.make_async_copy(hid, own_block, one.at[R_OWN]).start()
@@ -161,12 +160,15 @@
 
     def near_hidden():
         landed(rows_all.at[0, pl.ds(0, 2), 0], one.at[R_HZ])
-        for source, device, first in ((down_z, up_z, 0), (up_z, down_z, own // 2)):
-            piece = rows_all.at[0, source, c, pl.ds(first, own // 2)]
-            remote(piece, piece, S_HFAR, one.at[R_HFAR], {"z": device}).start()
         for source in (down_z, up_z):
             block = rows_all.at[0, source, c]
             remote(block, block, S_HC, one.at[R_HC], {"c": other}).start()
+
+    def hidden_on(part):
+        quarter = own // 4
+        for source, device, first in ((down_z, up_z, 0), (up_z, down_z, 2)):
+            piece = rows_all.at[0, source, c, pl.ds((first + part) * quarter, quarter)]
+            remote(piece, piece, S_HFAR, one.at[R_HFAR], {"z": device}).start()
 
     def far_hidden():
         landed(rows_all.at[0, 0, 0], one.at[R_HFAR])
@@ -241,9 +243,10 @@
     events = 2 * (VOCAB_TILES + 1)
 
     def step(t, carry):
-        stages = ((LAG_X2, along_x2), (LAG_Y, along_y), (LAG_RELAY, relay_z), (LAG_Z, along_z),
-                  (LAG_FAR, far_x), (LAG_X, along_x), (LAG_SWAP, swap), (0, merge))
-        for lag, stage in stages:
+        stages = {"x2": (LAG_X2, along_x2), "y": (LAG_Y, along_y), "relay": (LAG_RELAY, relay_z),
+                  "z": (LAG_Z, along_z), "far_x": (LAG_FAR, far_x), "x": (LAG_X, along_x),
+                  "swap": (LAG_SWAP, swap), "merge": (0, merge)}
+        for lag, stage in (stages[name] for name in ORDER):
             k = t - lag
 
             @pl.when(jnp.logical_and(k >= 0, k < CHUNKS))
@@ -251,11 +254,13 @@
                 stage(k)
 
         pl.when(t == STEP_NEAR)(near_hidden)
+        pl.when(t == STEP_ON)(lambda: hidden_on(0))
+        pl.when(t == STEP_ON2)(lambda: hidden_on(1))
         pl.when(t == STEP_FAR)(far_hidden)
 
         piece = t - STEP_HIDDEN
 
-        @pl.when((piece >= 0) & (lax.rem(piece, EVERY) == 0) & (piece < 4 * PIECES * EVERY))
+        @pl.when((piece >= EARLY * EVERY) & (lax.rem(piece, EVERY) == 0) & (piece < 4 * PIECES * EVERY))
         def _():
             hidden_y(piece // EVERY)
 
@@ -324,7 +329,9 @@
               for i in range(WRITES)]
     for copy in copies:
         copy.start()
-    both_out[...] = both[...]
+    values = both[...]
+    mine = jnp.where(lax.axis_index("c") == 0, values, pltpu.roll(values, LANES // 2, 1))
+    both_out[...] = mine[:, : LANES // 2]
     for copy in copies:
         copy.wait()
 
@@ -369,18 +376,17 @@
             collective_id=0, has_side_effects=True, vmem_limit_bytes=40 * 2**20
         ),
     )(*(pltpu.with_memory_space_constraint(a, pltpu.HBM) for a in (hidden, tokens.reshape(8, LANES), old_weight, new_weight.T)))
-    engine_weight, both = pl.pallas_call(
+    engine_weight, logprob = pl.pallas_call(
         write_out,
         out_shape=(
             jax.ShapeDtypeStruct((vocab_rows, width), jnp.bfloat16),
-            jax.ShapeDtypeStruct((1, LANES), jnp.float32),
+            jax.ShapeDtypeStruct((1, own), jnp.float32),
         ),
         in_specs=[pl.BlockSpec(memory_space=pl.ANY), pl.BlockSpec(memory_space=pltpu.VMEM)],
         out_specs=(pl.BlockSpec(memory_space=pl.ANY), pl.BlockSpec(memory_space=pltpu.VMEM)),
         scratch_shapes=[sems((WRITES,))],
         compiler_params=pltpu.CompilerParams(vmem_limit_bytes=2**20),
     )(engine_weight, both)
-    logprob = lax.dynamic_slice(both, (0, lax.axis_index("c") * own), (1, own))
     return logprob.reshape(own), engine_weight
 
 

time: 120 us -> 115 us (0.958)
  Pallas kernels: 118 us -> 115 us
    pallas_call x1, Pallas kernels: 114 us -> 110 us  [on_device(): pl.pallas_call(kernel, out_shape=(pltpu.VMEM((vocab_rows, width), jnp.bfl...]
where the time goes in v3:
time: 115 us
  Pallas kernels  115 us (100%)
    pallas_call x1, Pallas kernels, on_device(): pl.pallas_call(kernel, out_shape=(pltpu.VMEM((vocab_rows, width), jnp.bfl...  110 us
    pallas_call x1, Pallas kernels, on_device(): pl.pallas_call(write_out, out_shape=(jax.ShapeDtypeStruct((vocab_rows, wi...  4.92 us

profile of v3, /device:TPU:1, one launch (start us, length us, event | category | flops | bytes accessed | tf_op | source)
XLA Modules:
  0.0 115.4 jit_solution(14711329026051897762)
XLA Ops:
  0.6 109.8 %shard_map.59 = (bf16[1152,5120]{1,0:T(8,128)(2,1)S(1)}, f32[1,128]{1,0:T(1,128)S(1)}) custom-call(bf16[64,5120]{1,0:T(8,128)(2,1)} %hid.1, s32[8,128]{1,0:T(8,128)} %bitcast.4, bf16[1152,5120]{1,0:T(8,128)(2,1)} %old.1, bf16[320,2304]{1,0:T(8,128)(2,1)} %bitcast.3), custom_call_target="tpu_custom_call" | custom-call | tf_op jit(solution)/shard_map/pallas_call | solution.py:344
  110.4 4.9 %shard_map.60 = (bf16[1152,5120]{1,0:T(8,128)(2,1)}, f32[1,64]{1,0:T(1,128)}) custom-call(bf16[1152,5120]{1,0:T(8,128)(2,1)S(1)} %get-tuple-element.6.held, f32[1,128]{1,0:T(1,128)S(1)} %get-tuple-element.7.both), custom_call_target="tpu_custom_call" | custom-call | tf_op jit(solution)/shard_map/pallas_call | solution.py:379

commit v4 on v3

--- a/solution.py
+++ b/solution.py
@@ -14,19 +14,19 @@
 MESH = pl.DeviceIdType.MESH
 
 CHUNKS = 18
-HALVES = 3
+HALVES = 9
 BLOCK = 128
 LAG_SWAP, LAG_X, LAG_FAR, LAG_Z, LAG_RELAY, LAG_Y, LAG_X2 = 2, 10, 13, 15, 17, 19, 24
 ORDER = ("merge", "far_x", "x2", "y", "swap", "x", "relay", "z")
 STEP_NEAR, STEP_ON, STEP_ON2, STEP_FAR, STEP_OWN, STEP_OTHER = 11, 11, 12, 16, 17, 25
 STEP_HIDDEN, EVERY, STEP_ARRIVED = 12, 1, 24
-EARLY = 2
+EARLY = 1
 PIECES = 4
 PERIOD = PIECES * EVERY
 VOCAB_TILES = 3
 STEPS = max(CHUNKS + LAG_X2, STEP_OTHER + 3 * PERIOD + VOCAB_TILES + 1)
 LANES = 128
-WRITES = 8
+WRITES = 4
 
 (S_HALF, S_SWAP, S_X, S_FAR, S_Z, S_RELAY, S_Y, S_X2, S_HZ, S_HFAR, S_HC, S_HY, S_HC2,
  S_TOK, S_STAT, N_SEND) = range(16)

time: 115 us -> 116 us (level)
  no operation moved by 1% of the time
where the time goes in v4:
time: 116 us; the launch traced here: 115 us
  Pallas kernels  115 us (99%)
    pallas_call x1, Pallas kernels, on_device(): pl.pallas_call(kernel, out_shape=(pltpu.VMEM((vocab_rows, width), jnp.bfl...  110 us
    pallas_call x1, Pallas kernels, on_device(): pl.pallas_call(write_out, out_shape=(jax.ShapeDtypeStruct((vocab_rows, wi...  4.97 us

profile of v4, /device:TPU:1, one launch (start us, length us, event | category | flops | bytes accessed | tf_op | source)
XLA Modules:
  0.0 115.5 jit_solution(5216301664479554432)
XLA Ops:
  0.6 109.9 %shard_map.59 = (bf16[1152,5120]{1,0:T(8,128)(2,1)S(1)}, f32[1,128]{1,0:T(1,128)S(1)}) custom-call(bf16[64,5120]{1,0:T(8,128)(2,1)} %hid.1, s32[8,128]{1,0:T(8,128)} %bitcast.4, bf16[1152,5120]{1,0:T(8,128)(2,1)} %old.1, bf16[320,2304]{1,0:T(8,128)(2,1)} %bitcast.3), custom_call_target="tpu_custom_call" | custom-call | tf_op jit(solution)/shard_map/pallas_call | solution.py:344
  110.5 5.0 %shard_map.60 = (bf16[1152,5120]{1,0:T(8,128)(2,1)}, f32[1,64]{1,0:T(1,128)}) custom-call(bf16[1152,5120]{1,0:T(8,128)(2,1)S(1)} %get-tuple-element.6.held, f32[1,128]{1,0:T(1,128)S(1)} %get-tuple-element.7.both), custom_call_target="tpu_custom_call" | custom-call | tf_op jit(solution)/shard_map/pallas_call | solution.py:379
